TPU v7x, 16 devices: a 4x2x1 block of a 4x4x8 slice. The times are simulated.
16 devices in a mesh: rep: 2 (over y, z), dp: 8 (over x, core).
Axes of the slice: x: 4, y: 2, z: 1, core: 2. Of those that a mesh axis runs over, the one named last changes fastest.
The devices are a block of a 4x4x8 slice.
Arguments:
- x: bfloat16 [16, 2048, 1024], P(('rep', 'dp')), parts along dimension 0
- dy: bfloat16 [16, 2048, 1024], P(('rep', 'dp')), parts along dimension 0
- w_gate: bfloat16 [2, 1024, 4096], P(None, 'dp')
- w_up: bfloat16 [2, 1024, 4096], P(None, 'dp')
- w_down: bfloat16 [2, 4096, 1024], P(None, 'dp')
- m_w_gate: float32 [2, 1024, 4096], P(None, 'dp')
- m_w_up: float32 [2, 1024, 4096], P(None, 'dp')
- m_w_down: float32 [2, 4096, 1024], P(None, 'dp')
- v_w_gate: float32 [2, 1024, 4096], P(None, 'dp')
- v_w_up: float32 [2, 1024, 4096], P(None, 'dp')
- v_w_down: float32 [2, 4096, 1024], P(None, 'dp')
Outputs:
- output 1: bfloat16 [4, 1024, 4096], P('rep', 'dp'), parts along dimension 0
- output 2: bfloat16 [4, 1024, 4096], P('rep', 'dp'), parts along dimension 0
- output 3: bfloat16 [4, 4096, 1024], P('rep', 'dp'), parts along dimension 0
- output 4: float32 [4, 1024, 4096], P('rep', 'dp'), parts along dimension 0
- output 5: float32 [4, 1024, 4096], P('rep', 'dp'), parts along dimension 0
- output 6: float32 [4, 4096, 1024], P('rep', 'dp'), parts along dimension 0
- output 7: float32 [4, 1024, 4096], P('rep', 'dp'), parts along dimension 0
- output 8: float32 [4, 1024, 4096], P('rep', 'dp'), parts along dimension 0
- output 9: float32 [4, 4096, 1024], P('rep', 'dp'), parts along dimension 0
There are 2 independent parts. A program takes and returns all parts, laid end to end along the dimension named above; an argument that names none is the same for every part.
All inputs are finite; a program needn't handle non-finite values.
Results may differ from a plain program's by a relative error of at most 0.022.
Values are sent between devices in bfloat16 or wider.
A program may use at most 768 MiB of HBM per device.

v0:
```python
import jax
import jax.numpy as jnp
from jax import lax
from jax.sharding import PartitionSpec as P

NAMES = ("w_gate", "w_up", "w_down")


def matmul(a, w):
    return jnp.dot(a, w, preferred_element_type=jnp.float32).astype(jnp.bfloat16)


def normed(h):
    wide = h.astype(jnp.float32)
    scale = lax.rsqrt(jnp.mean(wide**2, -1, keepdims=True) + 1e-6)
    return (wide * scale).astype(jnp.bfloat16)


def layer(h, w):
    a = normed(h)
    gate = jnp.dot(a, w["w_gate"], preferred_element_type=jnp.float32)
    up = jnp.dot(a, w["w_up"], preferred_element_type=jnp.float32)
    return h + matmul((jax.nn.silu(gate) * up).astype(jnp.bfloat16), w["w_down"])


def adamw(w, m, v, g):
    m = 0.9 * m + 0.1 * g
    v = 0.95 * v + 0.05 * g * g
    step = m * lax.rsqrt(v + 1e-8) + 0.1 * w
    return (w - 0.02 * step).astype(jnp.bfloat16), m, v


def solution(mesh):
    def fetched(weights, number):
        return {name: lax.all_gather(w[number], "dp", axis=0, tiled=True) for name, w in zip(NAMES, weights, strict=True)}

    def step(x, dy, *arrays):
        weights, m, v = (arrays[i : i + 3] for i in (0, 3, 6))
        layers = weights[0].shape[0]
        h, kept = x[0], []
        for number in range(layers):
            kept.append(h)
            h = layer(h, fetched(weights, number))
        by_h, mine = dy[0], [None] * layers
        for number in reversed(range(layers)):
            _, back = jax.vjp(lambda w, h: layer(h, w), fetched(weights, number), kept[number])
            by_w, by_h = back(by_h)
            mine[number] = [lax.psum_scatter(by_w[name], "dp", scatter_dimension=0, tiled=True) for name in NAMES]
        gradients = [jnp.stack([mine[number][i] for number in range(layers)]).astype(jnp.float32) for i in range(3)]
        new = [adamw(w.astype(jnp.float32), m, v, g) for w, m, v, g in zip(weights, m, v, gradients, strict=True)]
        return tuple(one[which] for which in range(3) for one in new)

    states, cut = P(("rep", "dp"), None, None), P(None, "dp", None)
    return jax.shard_map(
        step,
        mesh=mesh,
        in_specs=(states, states) + (cut,) * 9,
        out_specs=(P("rep", "dp", None),) * 9,
        check_vma=False,
    )
```

profile of v0, /device:TPU:112, one launch (start us, length us, event | category | flops | bytes accessed | tf_op | source)
XLA Modules:
  0.0 741.0 jit_solution(3521630917927681301)
XLA Ops:
  33.3 25.6 %all-gather.13.cloned.1.call-done = bf16[1,1024,4096]{2,1,0:T(8,128)(2,1)} async-done(((bf16[1,128,4096]{2,1,0:T(8,128)(2,1)}), bf16[1,1024,4096]{2,1,0:T(8,128)(2,1)}) %all-gather.13.cloned.1.call-update) | async-done | bytes 8388624 | tf_op jit(solution)/shard_map/all_gather | solution.py:35
  59.0 24.4 %fusion.35 = f32[2048,4096]{1,0:T(8,128)} fusion(bf16[1,1024,4096]{2,1,0:T(8,128)(2,1)} %all-gather.13.cloned.1.call-done, bf16[1,2048,1024]{1,2,0:T(8,128)(2,1)} %copy.20, f32[2048]{0:T(1024)S(1)} %add_rsqrt_fusion), kind=kOutput, calls=%fused_computation.53 | convolution fusion | flops 17186160640 | bytes 46145536 | tf_op jit(solution)/shard_map/dot_general | solution.py:21
  83.4 23.5 %all-gather.15.cloned.1.call-done = bf16[1,1024,4096]{2,1,0:T(8,128)(2,1)} async-done(((bf16[1,128,4096]{2,1,0:T(8,128)(2,1)}), bf16[1,1024,4096]{2,1,0:T(8,128)(2,1)}) %all-gather.15.cloned.1.call-update) | async-done | bytes 8388624 | tf_op jit(solution)/shard_map/all_gather | solution.py:35
  106.8 39.2 %multiply_convert_fusion.1 = (bf16[2048,4096]{1,0:T(8,128)(2,1)}, f32[2048,4096]{1,0:T(8,128)}) fusion(f32[2048,4096]{1,0:T(8,128)} %fusion.35, bf16[1,1024,4096]{2,1,0:T(8,128)(2,1)} %all-gather.15.cloned.1.call-done, bf16[1,2048,1024]{1,2,0:T(8,128)(2,1)} %copy.20, f32[2048]{0:T(1024)S(1)} %add_rsqrt_fusion), kind=kOutput, calls=%fused_computation.17 | convolution fusion | flops 17236492288 | bytes 96477184 | tf_op jit(solution)/shard_map/dot_general | solution.py:22
  146.1 8.6 %all-gather.17.cloned.1.call-done = bf16[1,4096,1024]{2,1,0:T(8,128)(2,1)} async-done(((bf16[1,512,1024]{2,1,0:T(8,128)(2,1)}), bf16[1,4096,1024]{2,1,0:T(8,128)(2,1)}) %all-gather.17.cloned.1.call-update) | async-done | bytes 8388624 | tf_op jit(solution)/shard_map/all_gather | solution.py:35
  154.7 24.5 %fusion.19 = (f32[2048]{0:T(1024)S(1)}, bf16[2048,1024]{0,1:T(8,128)(2,1)}) fusion(bf16[2048,4096]{1,0:T(8,128)(2,1)} %get-tuple-element.24, bf16[1,4096,1024]{2,1,0:T(8,128)(2,1)} %all-gather.17.cloned.1.call-done, bf16[1,2048,1024]{1,2,0:T(8,128)(2,1)} %copy.20), kind=kOutput, calls=%fused_computation.37 | convolution fusion | flops 17190352896 | bytes 33562624 | tf_op jit(solution)/shard_map/dot_general | solution.py:10
  179.8 22.6 %all-gather.23.cloned.1.call-done = bf16[1,1024,4096]{2,1,0:T(8,128)(2,1)} async-done(((bf16[1,128,4096]{2,1,0:T(8,128)(2,1)}), bf16[1,1024,4096]{2,1,0:T(8,128)(2,1)}) %all-gather.23.cloned.1.call-update) | async-done | bytes 8388624 | tf_op jit(solution)/shard_map/all_gather | solution.py:35
  202.4 24.3 %fusion.22 = f32[2048,4096]{1,0:T(8,128)} fusion(bf16[1,1024,4096]{2,1,0:T(8,128)(2,1)} %all-gather.23.cloned.1.call-done, bf16[2048,1024]{0,1:T(8,128)(2,1)} %get-tuple-element.27, f32[2048]{0:T(1024)S(1)} %fusion.74), kind=kOutput, calls=%fused_computation.40 | convolution fusion | flops 17186160640 | bytes 46145536 | tf_op jit(solution)/shard_map/jvp()/dot_general | solution.py:22
  226.8 23.4 %all-gather.21.cloned.1.call-done = bf16[1,4096,1024]{2,1,0:T(8,128)(2,1)} async-done(((bf16[1,512,1024]{2,1,0:T(8,128)(2,1)}), bf16[1,4096,1024]{2,1,0:T(8,128)(2,1)}) %all-gather.21.cloned.1.call-update) | async-done | bytes 8388624 | tf_op jit(solution)/shard_map/all_gather | solution.py:35
  250.1 24.5 %convolution_convert_fusion.1 = bf16[2048,4096]{1,0:T(8,128)(2,1)} fusion(bf16[1,4096,1024]{2,1,0:T(8,128)(2,1)} %all-gather.21.cloned.1.call-done, bf16[1,2048,1024]{2,1,0:T(8,128)(2,1)} %param.12), kind=kOutput, calls=%fused_computation.25 | convolution fusion | flops 17188257792 | bytes 29360128 | tf_op jit(solution)/shard_map/transpose(jvp())/dot_general | solution.py:10
  274.6 23.3 %all-gather.19.cloned.1.call-done = bf16[1,1024,4096]{2,1,0:T(8,128)(2,1)} async-done(((bf16[1,128,4096]{2,1,0:T(8,128)(2,1)}), bf16[1,1024,4096]{2,1,0:T(8,128)(2,1)}) %all-gather.19.cloned.1.call-update) | async-done | bytes 8388624 | tf_op jit(solution)/shard_map/all_gather | solution.py:35
  297.9 46.5 %fusion.2 = (bf16[2048,4096]{1,0:T(8,128)(2,1)}, f32[2048,4096]{1,0:T(8,128)}) fusion(f32[2048,4096]{1,0:T(8,128)} %fusion.22, bf16[2048,4096]{1,0:T(8,128)(2,1)} %convolution_convert_fusion.1, bf16[1,1024,4096]{2,1,0:T(8,128)(2,1)} %all-gather.19.cloned.1.call-done, bf16[2048,1024]{0,1:T(8,128)(2,1)} %get-tuple-element.27, f32[2048]{0:T(1024)S(1)} %fusion.74), kind=kOutput, calls=%fused_computation.8 | convolution fusion | flops 17286823936 | bytes 113254400 | tf_op jit(solution)/shard_map/jvp()/dot_general | solution.py:21
  344.4 27.3 %fusion.12 = bf16[2048,1024]{0,1:T(8,128)(2,1)} fusion(bf16[2048,4096]{1,0:T(8,128)(2,1)} %convolution_convert_fusion.1, bf16[1,1024,4096]{2,1,0:T(8,128)(2,1)} %all-gather.23.cloned.1.call-done, f32[2048,4096]{1,0:T(8,128)} %get-tuple-element.29), kind=kOutput, calls=%fused_computation.21 | convolution fusion | flops 17230200832 | bytes 62914560 | tf_op jit(solution)/shard_map/transpose(jvp())/dot_general | solution.py:22
  371.6 25.1 %fusion.21 = (f32[2048]{0:T(1024)S(1)}, bf16[2048,1024]{0,1:T(8,128)(2,1)S(1)}) fusion(bf16[2048,1024]{0,1:T(8,128)(2,1)S(1)} %copy-done.4, bf16[2048,1024]{0,1:T(8,128)(2,1)} %fusion.12, bf16[2048,4096]{1,0:T(8,128)(2,1)} %get-tuple-element.28, bf16[1,1024,4096]{2,1,0:T(8,128)(2,1)} %all-gather.19.cloned.1.call-done), kind=kOutput, calls=%fused_computation.39 | convolution fusion | flops 17190352896 | bytes 37756928 | tf_op jit(solution)/shard_map/transpose(jvp())/dot_general | solution.py:21
  402.0 23.4 %convolution_convert_fusion.2 = bf16[4096,1024]{1,0:T(8,128)(2,1)} fusion(bf16[2048,4096]{1,0:T(8,128)(2,1)} %get-tuple-element.24, bf16[2048,1024]{0,1:T(8,128)(2,1)S(1)} %fusion.59), kind=kOutput, calls=%fused_computation.59 | convolution fusion | flops 17184063488 | bytes 29360128 | tf_op jit(solution)/shard_map/transpose(jvp())/dot_general | solution.py:10
  425.6 30.6 %fusion.40 = bf16[4096,1024]{1,0:T(8,128)(2,1)} fusion(f32[2048,4096]{1,0:T(8,128)} %fusion.22, bf16[1,2048,1024]{2,1,0:T(8,128)(2,1)} %param.12, f32[2048,4096]{1,0:T(8,128)} %get-tuple-element.29), kind=kOutput, calls=%fused_computation.56 | convolution fusion | flops 17234395136 | bytes 79691776 | tf_op jit(solution)/shard_map/transpose(jvp())/dot_general | solution.py:10
  456.3 24.9 %convolution_convert_fusion = bf16[2048,4096]{1,0:T(8,128)(2,1)} fusion(bf16[2048,1024]{0,1:T(8,128)(2,1)} %copy-done.5, bf16[1,4096,1024]{2,1,0:T(8,128)(2,1)} %all-gather.17.cloned.1.call-done), kind=kOutput, calls=%fused_computation.24 | convolution fusion | flops 17188257792 | bytes 29360128 | tf_op jit(solution)/shard_map/transpose(jvp())/dot_general | solution.py:10
  481.1 26.9 %fusion.42 = bf16[1024,4096]{1,0:T(8,128)(2,1)} fusion(bf16[2048,4096]{1,0:T(8,128)(2,1)} %convolution_convert_fusion, f32[2048,4096]{1,0:T(8,128)} %fusion.35, bf16[1,2048,1024]{1,2,0:T(8,128)(2,1)} %copy.20, f32[2048]{0:T(1024)S(1)} %copy-done.11), kind=kOutput, calls=%fused_computation.58 | convolution fusion | flops 17240686592 | bytes 62922752 | tf_op jit(solution)/shard_map/transpose(jvp())/dot_general | solution.py:22
  508.7 26.7 %fusion.41 = bf16[1024,4096]{1,0:T(8,128)(2,1)} fusion(bf16[2048,4096]{1,0:T(8,128)(2,1)} %convolution_convert_fusion.1, bf16[2048,1024]{0,1:T(8,128)(2,1)} %get-tuple-element.27, f32[2048]{0:T(1024)S(1)} %copy-done.7, f32[2048,4096]{1,0:T(8,128)} %get-tuple-element.29), kind=kOutput, calls=%fused_computation.57 | convolution fusion | flops 17240686592 | bytes 62922752 | tf_op jit(solution)/shard_map/transpose(jvp())/dot_general | solution.py:22
  535.5 37.1 %fusion.37 = bf16[1024,4096]{1,0:T(8,128)(2,1)} fusion(f32[2048,4096]{1,0:T(8,128)} %fusion.35, f32[2048,4096]{1,0:T(8,128)} %get-tuple-element.25, bf16[2048,4096]{1,0:T(8,128)(2,1)} %convolution_convert_fusion, bf16[1,2048,1024]{1,2,0:T(8,128)(2,1)} %copy.20, f32[2048]{0:T(1024)S(1)} %copy-done.11), kind=kOutput, calls=%fused_computation.55 | convolution fusion | flops 17282629632 | bytes 96477184 | tf_op jit(solution)/shard_map/transpose(jvp())/dot_general | solution.py:21
  572.8 23.1 %convolution_convert_fusion.3 = bf16[1024,4096]{1,0:T(8,128)(2,1)} fusion(bf16[2048,4096]{1,0:T(8,128)(2,1)} %get-tuple-element.28, bf16[2048,1024]{0,1:T(8,128)(2,1)} %get-tuple-element.27, f32[2048]{0:T(1024)S(1)} %copy-done.7), kind=kOutput, calls=%fused_computation.60 | convolution fusion | flops 17186160640 | bytes 29368320 | tf_op jit(solution)/shard_map/transpose(jvp())/dot_general | solution.py:21
  605.2 20.1 %reduce-scatter.13.cloned.1.call-done = bf16[128,4096]{1,0:T(8,128)(2,1)} async-done(((bf16[1024,4096]{1,0:T(8,128)(2,1)}), bf16[128,4096]{1,0:T(8,128)(2,1)}) %reduce-scatter.13.cloned.1.call-update) | async-done | bytes 1048592 | tf_op jit(solution)/shard_map/reduce_scatter | solution.py:48
  633.6 42.2 %reduce-scatter.7.cloned.1.call-done = bf16[128,4096]{1,0:T(8,128)(2,1)} async-done(((bf16[1024,4096]{1,0:T(8,128)(2,1)}), bf16[128,4096]{1,0:T(8,128)(2,1)}) %reduce-scatter.7.cloned.1.call-update) | async-done | bytes 1048592 | tf_op jit(solution)/shard_map/reduce_scatter | solution.py:48
  675.8 50.3 %reduce-scatter.9.cloned.1.call-done = bf16[128,4096]{1,0:T(8,128)(2,1)} async-done(((bf16[1024,4096]{1,0:T(8,128)(2,1)}), bf16[128,4096]{1,0:T(8,128)(2,1)}) %reduce-scatter.9.cloned.1.call-update) | async-done | bytes 1048592 | tf_op jit(solution)/shard_map/reduce_scatter | solution.py:48
  (64 shorter events, 58.1 us)
Async XLA Ops:
  7.2 6.6 copy-start.1
  7.2 51.8 %all-gather.13.cloned.1.call-start = ((), (), s32[]{:S(2)}) async-start(), calls=%async_computation.12 | async-start | bytes 9437184 | tf_op jit(solution)/shard_map/all_gather | solution.py:35
  10.5 96.3 %all-gather.15.cloned.1.call-start = ((), (), s32[]{:S(2)}) async-start(), calls=%async_computation.13 | async-start | bytes 9437184 | tf_op jit(solution)/shard_map/all_gather | solution.py:35
  13.8 141.0 %all-gather.17.cloned.1.call-start = ((), (), s32[]{:S(2)}) async-start(), calls=%async_computation.14 | async-start | bytes 9437184 | tf_op jit(solution)/shard_map/all_gather | solution.py:35
  15.4 187.0 %all-gather.23.cloned.1.call-start = ((), (), s32[]{:S(2)}) async-start(), calls=%async_computation.17 | async-start | bytes 9437184 | tf_op jit(solution)/shard_map/all_gather | solution.py:35
  16.0 234.1 %all-gather.21.cloned.1.call-start = ((), (), s32[]{:S(2)}) async-start(), calls=%async_computation.16 | async-start | bytes 9437184 | tf_op jit(solution)/shard_map/all_gather | solution.py:35
  16.7 281.2 %all-gather.19.cloned.1.call-start = ((), (), s32[]{:S(2)}) async-start(), calls=%async_computation.15 | async-start | bytes 9437184 | tf_op jit(solution)/shard_map/all_gather | solution.py:35
  17.3 578.7 %reduce-scatter.15.cloned.1.call-start = ((), (), s32[]{:S(2)}) async-start(), calls=%async_computation.10 | async-start | bytes 9437184 | tf_op jit(solution)/shard_map/reduce_scatter | solution.py:48
  26.9 80.0 %copy-start.10 = (f32[2048]{0:T(1024)}, f32[2048]{0:T(1024)S(1)}, u32[]{:S(2)}) copy-start(f32[2048]{0:T(1024)S(1)} %add_rsqrt_fusion) | copy-start | bytes 24580
  179.2 0.6 copy-start.8
  179.8 217.0 %copy-start.6 = (f32[2048]{0:T(1024)}, f32[2048]{0:T(1024)S(1)}, u32[]{:S(2)}) copy-start(f32[2048]{0:T(1024)S(1)} %fusion.74) | copy-start | bytes 24580
  344.4 27.3 %copy-start.4 = (bf16[2048,1024]{0,1:T(8,128)(2,1)S(1)}, bf16[2048,1024]{0,1:T(8,128)(2,1)}, u32[]{:S(2)}) copy-start(bf16[2048,1024]{0,1:T(8,128)(2,1)} %get-tuple-element.27) | copy-start | bytes 12582916
  371.6 25.1 %copy-start.9 = (f32[2048]{0:T(1024)S(1)}, f32[2048]{0:T(1024)}, u32[]{:S(2)}) copy-start(f32[2048]{0:T(1024)} %copy-done.8) | copy-start | bytes 24580
  371.6 25.2 %copy-start = (bf16[1,2048,1024]{1,2,0:T(8,128)(2,1)S(1)}, bf16[1,2048,1024]{1,2,0:T(8,128)(2,1)}, u32[]{:S(2)}) copy-start(bf16[1,2048,1024]{1,2,0:T(8,128)(2,1)} %copy.21) | copy-start | bytes 12582916
  400.0 2.0 copy-start.5
  425.5 170.5 %reduce-scatter.17.cloned.1.call-start = ((), (), s32[]{:S(2)}) async-start(), calls=%async_computation.11 | async-start | bytes 9437184 | tf_op jit(solution)/shard_map/reduce_scatter | solution.py:48
  456.2 24.9 %copy-start.11 = (f32[2048]{0:T(1024)S(1)}, f32[2048]{0:T(1024)}, u32[]{:S(2)}) copy-start(f32[2048]{0:T(1024)} %copy-done.10) | copy-start | bytes 24580
  456.2 149.0 %reduce-scatter.11.cloned.1.call-start = ((), (), s32[]{:S(2)}) async-start(), calls=%async_computation.8 | async-start | bytes 9437184 | tf_op jit(solution)/shard_map/reduce_scatter | solution.py:48
  508.0 0.7 copy-start.7
  508.1 117.3 %reduce-scatter.13.cloned.1.call-start = ((), (), s32[]{:S(2)}) async-start(), calls=%async_computation.9 | async-start | bytes 9437184 | tf_op jit(solution)/shard_map/reduce_scatter | solution.py:48
  535.5 140.3 %reduce-scatter.7.cloned.1.call-start = ((), (), s32[]{:S(2)}) async-start(), calls=%async_computation.6 | async-start | bytes 9437184 | tf_op jit(solution)/shard_map/reduce_scatter | solution.py:48
  572.7 153.3 %reduce-scatter.9.cloned.1.call-start = ((), (), s32[]{:S(2)}) async-start(), calls=%async_computation.7 | async-start | bytes 9437184 | tf_op jit(solution)/shard_map/reduce_scatter | solution.py:48
  595.9 1.6 copy-start.2
  625.4 100.7 %copy-start.3 = (bf16[2,128,4096]{2,1,0:T(8,128)(2,1)S(1)}, bf16[2,128,4096]{2,1,0:T(8,128)(2,1)}, u32[]{:S(2)}) copy-start(bf16[2,128,4096]{2,1,0:T(8,128)(2,1)} %param.13) | copy-start | bytes 6291460
Sparse Core Ops, SparseCore 0:
  10.7 48.2 all-gather.12
  61.2 45.6 all-gather.14
  109.0 45.6 all-gather.16
  156.7 45.6 all-gather.22
  204.5 45.6 all-gather.20
  252.2 45.6 all-gather.18
  425.6 48.6 reduce-scatter.14
  476.6 48.0 reduce-scatter.16
  527.0 48.0 reduce-scatter.10
  577.2 48.0 reduce-scatter.12
  627.7 48.0 reduce-scatter.6
  677.9 48.0 reduce-scatter.8
where the time goes:
time: 751 us; the launch traced here: 741 us
  matrix products  428 us (57%)
  waiting for transfers between devices  242 us (32%)
  other arithmetic  29.8 us (4%)
  local copies, waits for them, and re-layouts  25.3 us (3%)
  between operations  14.9 us (2%)
    dot_general x5, matrix products, layer(): gate = jnp.dot(a, w['w_gate'], preferred_element_type=jnp.float32)  156 us
    dot_general x5, matrix products, layer(): up = jnp.dot(a, w['w_up'], preferred_element_type=jnp.float32)  144 us
    dot_general x5, matrix products, matmul(): jnp.dot(a, w, preferred_element_type=jnp.float32).astype(jnp.bfloat16)  128 us
    all_gather x6, waiting for transfers between devices, fetched(): lax.all_gather(w[number], 'dp', axis=0, tiled=True)  127 us
    reduce_scatter x6, waiting for transfers between devices, step(): lax.psum_scatter(by_w[name], 'dp', scatter_dimension=0, tiled=True)  113 us
    convert_element_type x3, other arithmetic, adamw(): return ((w - 0.02 * step).astype(jnp.bfloat16), m, v)  23.6 us
    unnamed x26, local copies, waits for them, and re-layouts  17.5 us
  transfers between devices with their start and end apart: 12, of which 9 were waited for; matrix products, arithmetic and copies ran while one was open for 46% of the time, Pallas kernels for 0%

commit v1 on v0

v1 whole, which is shorter than its diff:
```python
import functools

import jax
import jax.numpy as jnp
from jax import lax
from jax.experimental import pallas as pl
from jax.experimental.pallas import tpu as pltpu
from jax.sharding import PartitionSpec as P

NAMES = ("w_gate", "w_up", "w_down")
MESH = pl.DeviceIdType.MESH
F32, BF16 = jnp.float32, jnp.bfloat16
R = 128
CH = 512
BM = 512
EPS = 1e-6
COMM = True
COMPUTE = True


def nn(a, b):
    return jnp.dot(a, b, preferred_element_type=F32)


def nt(a, b):
    return lax.dot_general(a, b, (((1,), (1,)), ((), ())), preferred_element_type=F32)


def tn(a, b):
    return lax.dot_general(a, b, (((0,), (0,)), ((), ())), preferred_element_type=F32)


def kernel(
    chips, layers, groups, x, dy, own, gout, agb, part, save,
    A0, A1, H, DY, ACC, WGU, WD, HID, DG, DU, ST, DWS, DWD, R0, PB, C, F, Q, G,
    in_sem, ag_send, ag_relay, ag_l, ag_r, ag_o, ag_p, ag_loc, w_sem, st_sem, dw_sem,
    s0, r0, lp, ss, rc, rf, g_sem, credit0, credit_l, credit_r,
):
    tokens, d = x.shape
    per_layer = 3 * groups
    packets = layers * per_layer
    chunks = 2 * groups
    me = lax.axis_index("dp")
    X, c = me // 2, lax.rem(me, 2)
    XR, XL, XO = lax.rem(X + 1, chips), lax.rem(X + chips - 1, chips), lax.rem(X + 2, chips)
    right, left, partner = {"dp": 2 * XR + c}, {"dp": 2 * XL + c}, {"dp": 2 * X + 1 - c}

    def remote(src, dst, send, recv, to):
        return pltpu.make_async_remote_copy(src_ref=src, dst_ref=dst, send_sem=send, recv_sem=recv, device_id=to, device_id_type=MESH)

    local = pltpu.make_async_copy

    def when(cond):
        if isinstance(cond, bool):
            return (lambda f: f()) if cond else (lambda f: None)
        return pl.when(cond)

    def e0(p):
        for to, sem in ((right, ag_l), (left, ag_r), (partner, ag_p)):
            remote(own.at[p], agb.at[p, X, c], ag_send.at[p], sem.at[p], to).start()
        local(own.at[p], agb.at[p, X, c], ag_loc.at[p]).start()

    def e1(p):
        remote(agb.at[p, XL, c], agb.at[p, XL, c], ag_send.at[p], ag_l.at[p], right).wait_recv()
        remote(agb.at[p, XL, c, 0], agb.at[p, XL, c, 0], ag_send.at[p], ag_o.at[p], right).start()
        remote(agb.at[p, XL, c], agb.at[p, XL, c], ag_relay.at[p], ag_p.at[p], partner).start()
        remote(agb.at[p, XR, c], agb.at[p, XR, c], ag_send.at[p], ag_r.at[p], left).wait_recv()
        remote(agb.at[p, XR, c, 1], agb.at[p, XR, c, 1], ag_send.at[p], ag_o.at[p], left).start()
        remote(agb.at[p, XR, c], agb.at[p, XR, c], ag_relay.at[p], ag_p.at[p], partner).start()

    def e2(p):
        remote(agb.at[p, XO, c], agb.at[p, XO, c], ag_relay.at[p], ag_o.at[p], partner).wait_recv()
        remote(agb.at[p, XO, c], agb.at[p, XO, c], ag_relay.at[p], ag_p.at[p], partner).start()

    def ready(p):
        if not COMM:
            return
        everyone = agb.at[p, :, 1 - c]
        remote(everyone, everyone, ag_relay.at[p], ag_p.at[p], partner).wait_recv()
        local(own.at[p], agb.at[p, X, c], ag_loc.at[p]).wait()

    def ag_tick(a):
        if not COMM:
            return
        when(a < packets)(lambda: e0(a))
        when((a >= 2) & (a < packets + 2) if not isinstance(a, int) else 2 <= a < packets + 2)(lambda: e1(a - 2))
        when((a >= 3) & (a < packets + 3) if not isinstance(a, int) else 3 <= a < packets + 3)(lambda: e2(a - 3))

    def ag_drain():
        if not COMM:
            return

        @pl.loop(0, packets)
        def _(p):
            four, three = agb.at[p, :, 0], agb.at[p, pl.ds(0, 3), 0]
            remote(four, four, ag_send.at[p], ag_p.at[p], partner).wait_send()
            remote(three, three, ag_relay.at[p], ag_p.at[p], partner).wait_send()

    def rs0(t):
        s = lax.rem(t, 4)
        pl.when(t >= 4)(lambda: pl.semaphore_wait(credit0, 1))
        remote(part.at[t, :, 1 - c], R0.at[s], s0.at[s], r0.at[s], partner).start()
        local(part.at[t, :, c], PB.at[s], lp.at[s]).start()

    def plus(out, *terms):
        total = terms[0][...].astype(F32)
        for term in terms[1:]:
            total += term[...].astype(F32)
        out[...] = total.astype(BF16)

    def firsts(s):
        return (
            (PB.at[s, XO, 0], C.at[s, 0], ss.at[s, 0], rc.at[s, 0], right),
            (PB.at[s, XO, 1], C.at[s, 1], ss.at[s, 1], rc.at[s, 1], left),
            (PB.at[s, XR, 1], F.at[s, 0], ss.at[s, 2], rf.at[s, 0], right),
            (PB.at[s, XL, 0], F.at[s, 1], ss.at[s, 3], rf.at[s, 1], left),
        )

    def seconds(s):
        return (
            (Q.at[s, 0], F.at[s, 2], ss.at[s, 4], rf.at[s, 2], right),
            (Q.at[s, 1], F.at[s, 3], ss.at[s, 5], rf.at[s, 3], left),
        )

    def rs1(t):
        s = lax.rem(t, 4)
        remote(part.at[t, :, 1 - c], R0.at[s], s0.at[s], r0.at[s], partner).wait_recv()
        local(part.at[t, :, c], PB.at[s], lp.at[s]).wait()

        @pl.when(t >= 4)
        def _():
            pl.semaphore_wait(credit_l, 1)
            pl.semaphore_wait(credit_r, 1)

        @pl.loop(0, 2 * chips)
        def _(b):
            y, h = b // 2, lax.rem(b, 2)
            plus(PB.at[s, y, h], PB.at[s, y, h], R0.at[s, y, h])

        pl.when(t + 4 < packets)(lambda: pl.semaphore_signal(credit0, 1, device_id=partner, device_id_type=MESH))
        for send in firsts(s):
            remote(*send).start()

    def rs2(t):
        s = lax.rem(t, 4)
        for send in firsts(s)[:2]:
            remote(*send).wait_recv()
        plus(Q.at[s, 0], PB.at[s, XR, 0], C.at[s, 0])
        plus(Q.at[s, 1], PB.at[s, XL, 1], C.at[s, 1])
        for send in seconds(s):
            remote(*send).start()

    def rs3(t):
        s, g = lax.rem(t, 4), lax.rem(t, 2)
        for send in firsts(s)[2:] + seconds(s):
            remote(*send).wait_recv()
        pl.when(t >= 2)(lambda: local(G.at[g], gout.at[t - 2], g_sem.at[g]).wait())
        plus(G.at[g, 0], PB.at[s, X, 0], F.at[s, 1], F.at[s, 2])
        plus(G.at[g, 1], PB.at[s, X, 1], F.at[s, 0], F.at[s, 3])
        local(G.at[g], gout.at[t], g_sem.at[g]).start()
        for send in firsts(s) + seconds(s):
            remote(*send).wait_send()
        remote(part.at[t, :, 1 - c], R0.at[s], s0.at[s], r0.at[s], partner).wait_send()

        @pl.when(t + 4 < packets)
        def _():
            pl.semaphore_signal(credit_r, 1, device_id=left, device_id_type=MESH)
            pl.semaphore_signal(credit_l, 1, device_id=right, device_id_type=MESH)

    def rs_tick(k):
        if not COMM:
            return
        pl.when((k >= 0) & (k < packets))(lambda: rs0(k))
        pl.when((k >= 1) & (k < packets + 1))(lambda: rs1(k - 1))
        pl.when((k >= 2) & (k < packets + 2))(lambda: rs2(k - 2))
        pl.when((k >= 3) & (k < packets + 3))(lambda: rs3(k - 3))

    def p_down(layer, j):
        return layer * per_layer + 3 * (j // 2)

    def p_gu(layer, j):
        return p_down(layer, j) + 1 + lax.rem(j, 2)

    def gu_load(layer, j, slot):
        return local(agb.at[p_gu(layer, j)], WGU.at[slot], w_sem.at[slot, 0])

    def down_load(layer, j, slot):
        return local(agb.at[p_down(layer, j), :, lax.rem(j, 2)], WD.at[slot], w_sem.at[slot, 1])

    def w_in(slot, which):
        return WGU[slot, :, :, which].reshape(d, CH)

    def w_out(slot, half):
        return WD[slot, :, half].reshape(CH, CH)

    def normed(src, dst):
        @pl.loop(0, tokens // 256)
        def _(b):
            rows = pl.ds(pl.multiple_of(b * 256, 256), 256)
            wide = src[rows, :].astype(F32)
            scale = lax.rsqrt(jnp.mean(wide * wide, -1, keepdims=True) + EPS)
            dst[rows, :] = (wide * scale).astype(BF16)

    def rows_of(r):
        return pl.ds(pl.multiple_of(r * BM, BM), BM)

    blocks = tokens // BM

    def by_hidden(slot, rows):
        return nt(DY[rows, : d // 2], w_out(slot, 0)) + nt(DY[rows, d // 2 :], w_out(slot, 1))

    def through(gate, up, dh, rows):
        dh = dh.astype(BF16).astype(F32)
        sig = jax.nn.sigmoid(gate)
        act = gate * sig
        HID[rows, :] = (act * up).astype(BF16)
        DU[rows, :] = (dh * act).astype(BF16)
        DG[rows, :] = (dh * up * (sig * (1 + gate * (1 - sig)))).astype(BF16)

    def part_out(t):
        return local(DWS, part.at[t], dw_sem.at[0])

    def part_down(t, j):
        return local(DWD, part.at[t, :, lax.rem(j, 2)], dw_sem.at[1])

    def gradients(A, t, t_down, j):
        for half in range(2):
            g = tn(HID[...], DY[:, half * CH : (half + 1) * CH])
            DWD[:, half] = g.astype(BF16).reshape(chips, R, CH)
        part_down(t_down, j).start()
        for b in range(d // 256):
            cols = slice(256 * b, 256 * b + 256)
            for which, by in ((0, DG), (1, DU)):
                g = tn(A[:, cols], by[...])
                DWS[b, :, which] = g.astype(BF16).reshape(2, R, CH)
        part_out(t).start()

    def unit_gu(k):
        return 3 * (k // 2) + lax.rem(k, 2)

    def unit_down(k):
        return 3 * (k // 2) + 2

    def settle(k):
        part_out(unit_gu(k)).wait()
        part_down(unit_down(k), k).wait()

    if COMM:
        barrier = pltpu.get_barrier_semaphore()
        for to in (left, right, partner):
            pl.semaphore_signal(barrier, 1, device_id=to, device_id_type=MESH)
        pl.semaphore_wait(barrier, 3)
    load_x, load_dy = local(x, H, in_sem.at[0]), local(dy, DY, in_sem.at[1])
    load_x.start()
    load_dy.start()
    ag_tick(0)
    ag_tick(1)
    load_x.wait()
    normed(H, A0)
    ACC[...] = jnp.zeros_like(ACC)
    load_dy.wait()
    ag_tick(2)

    def saved(b, slot, out):
        if out:
            return local(ST.at[slot], save.at[b], st_sem.at[slot])
        return local(save.at[b], ST.at[slot], st_sem.at[slot])

    @pl.loop(0, chunks)
    def _(i):
        slot = lax.rem(i, 2)
        p = p_gu(0, i)

        @pl.when(slot == 0)
        def _():
            ag_tick(p + 2)
            ready(p - 1)

        ag_tick(p + 3)
        ready(p)
        if COMPUTE:
            gu_load(0, i, slot).start()
            down_load(0, i, slot).start()
            gu_load(0, i, slot).wait()
            down_load(0, i, slot).wait()

            @pl.loop(0, blocks)
            def _(r):
                rows = rows_of(r)
                b = i * blocks + r
                ss_ = lax.rem(b, 2)
                a = A0[rows, :]
                gate = nn(a, w_in(slot, 0))
                up = nn(a, w_in(slot, 1))
                pl.when(b >= 2)(lambda: saved(b - 2, ss_, True).wait())
                ST[ss_, 0] = gate
                ST[ss_, 1] = up
                saved(b, ss_, True).start()
                hid = (gate * jax.nn.sigmoid(gate) * up).astype(BF16)
                for half in range(2):
                    cols = slice(half * CH, half * CH + CH)
                    ACC[rows, cols] += nn(hid, w_out(slot, half))

    last = chunks * blocks
    if COMPUTE:
        for b in (last - 2, last - 1):
            saved(b, b % 2, True).wait()
    ag_tick(per_layer + 3)
    if COMPUTE:
        @pl.loop(0, tokens // 256)
        def _(b):
            rows = pl.ds(pl.multiple_of(b * 256, 256), 256)
            h = (H[rows, :].astype(F32) + ACC[rows, :].astype(BF16).astype(F32)).astype(BF16)
            H[rows, :] = h
            wide = h.astype(F32)
            scale = lax.rsqrt(jnp.mean(wide * wide, -1, keepdims=True) + EPS)
            A1[rows, :] = (wide * scale).astype(BF16)
            ACC[rows, :] = jnp.zeros((256, d), F32)
    ag_tick(per_layer + 4)
    ready(per_layer)
    ready(per_layer + 1)
    if COMPUTE:
        gu_load(1, 0, 0).start()
        down_load(1, 0, 0).start()

    @pl.loop(0, chunks)
    def _(i):
        slot = lax.rem(i, 2)
        if COMPUTE:
            gu_load(1, i, slot).wait()
            down_load(1, i, slot).wait()
        ag_tick(per_layer + 5 + 2 * i)

        @pl.when(i + 1 < chunks)
        def _():
            p = p_gu(1, i + 1)
            pl.when(slot == 1)(lambda: ready(p - 1))
            ready(p)
            if COMPUTE:
                gu_load(1, i + 1, 1 - slot).start()
                down_load(1, i + 1, 1 - slot).start()

        if COMPUTE:
            @pl.loop(0, blocks)
            def _(r):
                rows = rows_of(r)
                a = A1[rows, :]
                through(nn(a, w_in(slot, 0)), nn(a, w_in(slot, 1)), by_hidden(slot, rows), rows)
                ACC[rows, :] += nt(DG[rows, :], w_in(slot, 0)) + nt(DU[rows, :], w_in(slot, 1))

            pl.when(i >= 1)(lambda: settle(i - 1))
        pl.when(i >= 1)(lambda: rs_tick(unit_gu(i - 1)))
        ag_tick(per_layer + 6 + 2 * i)
        if COMPUTE:
            gradients(A1, unit_gu(i), unit_down(i), i)
        pl.when((i >= 1) & (slot == 0))(lambda: rs_tick(unit_down(i - 1)))

    if COMPUTE:
        down_load(0, 0, 0).start()
        for b in range(2):
            saved(b, b, False).start()

        @pl.loop(0, tokens // 256)
        def _(b):
            rows = pl.ds(pl.multiple_of(b * 256, 256), 256)
            wide = H[rows, :].astype(F32)
            by = ACC[rows, :].astype(BF16).astype(F32)
            scale = lax.rsqrt(jnp.mean(wide * wide, -1, keepdims=True) + EPS)
            inner = jnp.mean(by * wide, -1, keepdims=True)
            back = (by * scale - wide * (scale * scale * scale * inner)).astype(BF16)
            DY[rows, :] = (DY[rows, :].astype(F32) + back.astype(F32)).astype(BF16)

    @pl.loop(0, chunks)
    def _(i):
        slot = lax.rem(i, 2)
        k = chunks + i
        if COMPUTE:
            down_load(0, i, slot).wait()
            pl.when(i + 1 < chunks)(lambda: down_load(0, i + 1, 1 - slot).start())

            @pl.loop(0, blocks)
            def _(r):
                rows = rows_of(r)
                b = i * blocks + r
                ss_ = lax.rem(b, 2)
                saved(b, ss_, False).wait()
                through(ST[ss_, 0], ST[ss_, 1], by_hidden(slot, rows), rows)
                pl.when(b + 2 < last)(lambda: saved(b + 2, ss_, False).start())

            settle(k - 1)
        rs_tick(unit_gu(k - 1))
        if COMPUTE:
            gradients(A0, unit_gu(k), unit_down(k), i)
        pl.when(slot == 0)(lambda: rs_tick(unit_down(k - 1)))

    if COMPUTE:
        settle(2 * chunks - 1)

    @pl.loop(packets - 2, packets + 3)
    def _(k):
        rs_tick(k)

    if COMM:
        for t in (packets - 2, packets - 1):
            local(G.at[t % 2], gout.at[t], g_sem.at[t % 2]).wait()
    ag_drain()


def gradients_of(mesh, x, dy, own):
    chips = mesh.shape["dp"] // 2
    packets = own.shape[0]
    tokens, d = x.shape
    layers = 2
    groups = packets // layers // 3
    unit = (2, R, CH)
    dma, reg = pltpu.SemaphoreType.DMA, pltpu.SemaphoreType.REGULAR
    V = pltpu.VMEM
    chunks, blocks = 2 * groups, tokens // BM
    hbm = pl.BlockSpec(memory_space=pltpu.HBM)
    flops = 2 * tokens * d * (CH * chunks) * 15
    return pl.pallas_call(
        functools.partial(kernel, chips, layers, groups),
        out_shape=(
            jax.ShapeDtypeStruct((packets, *unit), BF16),
            jax.ShapeDtypeStruct((packets, chips, 2, *unit), BF16),
            jax.ShapeDtypeStruct((packets, chips, 2, *unit), BF16),
            jax.ShapeDtypeStruct((chunks * blocks, 2, BM, CH), F32),
        ),
        in_specs=[hbm] * 3,
        out_specs=(hbm,) * 4,
        scratch_shapes=[
            V((tokens, d), BF16), V((tokens, d), BF16), V((tokens, d), BF16), V((tokens, d), BF16), V((tokens, d), F32),
            V((2, chips, 2, *unit), BF16), V((2, chips, *unit), BF16),
            V((tokens, CH), BF16), V((tokens, CH), BF16), V((tokens, CH), BF16),
            V((2, 2, BM, CH), F32), V((chips, 2, *unit), BF16), V((chips, *unit), BF16),
            V((4, chips, *unit), BF16), V((4, chips, *unit), BF16), V((4, *unit), BF16), V((4, 4, R, CH), BF16), V((4, *unit), BF16),
            V((2, *unit), BF16),
            dma((2,)), *[dma((packets,))] * 7, dma((2, 2)), dma((2,)), dma((2,)),
            dma((4,)), dma((4,)), dma((4,)), dma((4, 6)), dma((4, 2)), dma((4, 4)), dma((2,)), reg, reg, reg,
        ],
        compiler_params=pltpu.CompilerParams(collective_id=0, has_side_effects=True, vmem_limit_bytes=67043328),
        cost_estimate=pl.CostEstimate(flops=flops, bytes_accessed=300 << 20, transcendentals=0),
        name="step",
    )(x, dy, own)[0]


def adamw(w, m, v, g):
    m = 0.9 * m + 0.1 * g
    v = 0.95 * v + 0.05 * g * g
    step = m * lax.rsqrt(v + 1e-8) + 0.1 * w
    return (w - 0.02 * step).astype(jnp.bfloat16), m, v


def solution(mesh):
    chips = mesh.shape["dp"] // 2

    def step(x, dy, *arrays):
        weights, m, v = (arrays[i : i + 3] for i in (0, 3, 6))
        layers, _, ff = weights[0].shape
        d = weights[2].shape[2]
        groups = ff // (2 * chips) // R

        def spread(w):
            return w.reshape(layers, R, chips, 2, groups, R).transpose(0, 4, 3, 1, 2, 5).reshape(layers, groups, 2, R, CH)

        gu = jnp.stack([spread(weights[0]), spread(weights[1])], 3)
        down = weights[2].reshape(layers, groups, R, 2, CH).transpose(0, 1, 3, 2, 4)
        own = jnp.concatenate([down[:, :, None], gu], 2).reshape(-1, 2, R, CH)
        g = gradients_of(mesh, x[0], dy[0], own).reshape(layers, groups, 3, 2, R, CH)[::-1]

        def gathered(which):
            return g[:, :, :2, which].reshape(layers, groups, 2, R, chips, R).transpose(0, 3, 4, 2, 1, 5).reshape(layers, R, ff)

        g_down = g[:, :, 2].transpose(0, 1, 3, 2, 4).reshape(layers, groups * R, d)
        gradients = [one.astype(jnp.float32) for one in (gathered(0), gathered(1), g_down)]
        new = [adamw(w.astype(jnp.float32), m, v, g) for w, m, v, g in zip(weights, m, v, gradients, strict=True)]
        return tuple(one[which] for which in range(3) for one in new)

    states, cut = P(("rep", "dp"), None, None), P(None, "dp", None)
    return jax.shard_map(
        step,
        mesh=mesh,
        in_specs=(states, states) + (cut,) * 9,
        out_specs=(P("rep", "dp", None),) * 9,
        check_vma=False,
    )
```

time: 751 us -> 665 us (0.89)
  Pallas kernels: 0 us -> 538 us
  matrix products: 428 us -> 0 us
  waiting for transfers between devices: 242 us -> 0 us
  local copies, waits for them, and re-layouts: 25.3 us -> 89.2 us
  between operations: 14.9 us -> 1.15 us
    pallas_call x0 -> x1, Pallas kernels: none -> 538 us  [gradients_of(): pl.pallas_call(functools.partial(kernel, chips, layers, groups), out_shap...]
    dot_general x15 -> x0, matrix products: 428 us -> none  [the longest x5 156 us: layer(): gate = jnp.dot(a, w['w_gate'], preferred_element_type=jnp.float32)]
    all_gather x6 -> x0, waiting for transfers between devices: 127 us -> none  [fetched(): lax.all_gather(w[number], 'dp', axis=0, tiled=True)]
    reduce_scatter x6 -> x0, waiting for transfers between devices: 113 us -> none  [step(): lax.psum_scatter(by_w[name], 'dp', scatter_dimension=0, tiled=True)]
    convert_element_type x0 -> x8, local copies, waits for them, and re-layouts: none -> 47.4 us  [step(): one.astype(jnp.float32)]
    reshape x0 -> x4, local copies, waits for them, and re-layouts: none -> 12 us  [the longest x2 7.12 us: spread(): w.reshape(layers, R, chips, 2, groups, R).transpose(0, 4, 3, 1, 2, 5)]
    unnamed x26, local copies, waits for them, and re-layouts: 17.5 us -> 7.72 us
    another operation x0 -> x2, local copies, waits for them, and re-layouts: none -> 8.2 us  [step(): gu = jnp.stack([spread(weights[0]), spread(weights[1])], 3)]
  transfers between devices with their start and end apart: 12 -> 0, of which waited for: 9 -> 0; matrix products, arithmetic and copies ran while one was open for 46% -> 0% of each run, Pallas kernels for 0% -> 0%
where the time goes in v1:
time: 665 us; the launch traced here: 658 us
  Pallas kernels  538 us (81%)
  local copies, waits for them, and re-layouts  89.2 us (13%)
  other arithmetic  30.1 us (5%)
    pallas_call x1, Pallas kernels, gradients_of(): pl.pallas_call(functools.partial(kernel, chips, layers, groups), out_shap...  538 us
    convert_element_type x8, local copies, waits for them, and re-layouts, step(): one.astype(jnp.float32)  47.4 us
    convert_element_type x3, other arithmetic, adamw(): return ((w - 0.02 * step).astype(jnp.bfloat16), m, v)  19.1 us

profile of v1, /device:TPU:112, one launch (start us, length us, event | category | flops | bytes accessed | tf_op | source)
XLA Modules:
  0.0 658.2 jit_solution(6628543095975455983)
XLA Ops:
  0.6 4.4 reshape.49
  5.1 4.1 copy.21
  9.1 4.1 stack_reshape.6
  13.2 2.7 reshape.50
  15.9 4.1 copy.22
  20.0 4.1 stack_reshape.7
  24.1 2.7 reshape.48
  26.9 2.2 copy.31
  29.7 4.3 maximum_maximum_fusion
  34.0 537.7 %step.1 = (bf16[24,2,128,512]{3,2,1,0:T(8,128)(2,1)}, bf16[24,4,2,2,128,512]{5,4,3,2,1,0:T(8,128)(2,1)}, bf16[24,4,2,2,128,512]{5,4,3,2,1,0:T(8,128)(2,1)}, f32[32,2,512,512]{3,2,1,0:T(8,128)}) custom-call(bf16[2048,1024]{1,0:T(8,128)(2,1)} %bitcast.34, bf16[2048,1024]{1,0:T(8,128)(2,1)} %bitcast.35, bf16[24,2,128,512]{3,2,1,0:T(8,128)(2,1)} %bitcast.31), custom_call_target="tpu_custom_call" | custom-call | flops 257698037760 | bytes 314572800 | tf_op jit(solution)/shard_map/step/pallas_call | solution.py:421
  571.7 1.7 slice.26
  573.5 3.9 fusion.15
  578.0 5.3 copy.25
  583.2 6.9 %reshape.55 = f32[2,512,1024]{2,1,0:T(8,128)} reshape(f32[2,4,128,2,512]{4,3,2,1,0:T(2,128)} %copy.25) | data formatting | bytes 8388608 | tf_op jit(solution)/shard_map/convert_element_type | solution.py:475
  590.1 6.2 reverse_convert_fusion
  596.3 5.2 reshape.57
  601.5 6.9 %copy.29 = f32[2,4,2,128,4,128]{5,1,2,4,3,0:T(4,128)} copy(f32[2,4,2,128,4,128]{5,4,3,2,1,0:T(4,128)} %reshape.57) | data formatting | bytes 8388608 | tf_op jit(solution)/shard_map/convert_element_type | solution.py:475
  608.4 5.5 reshape.54
  613.9 5.2 reshape.56
  619.1 6.9 %copy.30 = f32[2,4,2,128,4,128]{5,1,2,4,3,0:T(4,128)} copy(f32[2,4,2,128,4,128]{5,4,3,2,1,0:T(4,128)} %reshape.56) | data formatting | bytes 8388608 | tf_op jit(solution)/shard_map/convert_element_type | solution.py:475
  626.0 5.6 reshape.53
  631.6 8.7 %fusion.2 = (bf16[2,128,4096]{2,1,0:T(8,128)(2,1)}, f32[2,128,4096]{2,1,0:T(8,128)}, f32[2,128,4096]{2,1,0:T(8,128)}) fusion(bf16[2,128,4096]{2,1,0:T(8,128)(2,1)S(1)} %copy-done.2, f32[2,128,4096]{2,1,0:T(8,128)} %reshape.53, f32[2,128,4096]{2,1,0:T(8,128)} %param.19, f32[2,128,4096]{2,1,0:T(8,128)} %param.16), kind=kLoop, calls=%fused_computation.12 | loop fusion | flops 15728640 | bytes 25165824 | tf_op jit(solution)/shard_map/convert_element_type | solution.py:451
  644.2 5.6 fusion.5
  653.0 4.7 fusion.8
  (27 shorter events, 8.3 us)
Async XLA Ops:
  5.1 8.2 %copy-start.3 = (bf16[2,128,4096]{2,1,0:T(8,128)(2,1)S(1)}, bf16[2,128,4096]{2,1,0:T(8,128)(2,1)}, u32[]{:S(2)}) copy-start(bf16[2,128,4096]{2,1,0:T(8,128)(2,1)} %param.14) | copy-start | bytes 6291460
  15.9 8.2 %copy-start.5 = (bf16[2,512,1024]{2,1,0:T(8,128)(2,1)S(1)}, bf16[2,512,1024]{2,1,0:T(8,128)(2,1)}, u32[]{:S(2)}) copy-start(bf16[2,512,1024]{2,1,0:T(8,128)(2,1)} %param.15) | copy-start | bytes 6291460
  26.9 2.2 copy-start.7
  26.9 2.9 copy-start.8
  626.0 5.6 copy-start.2
  631.6 8.9 %copy-start.1 = (f32[2,128,4096]{2,1,0:T(8,128)S(1)}, f32[2,128,4096]{2,1,0:T(8,128)}, u32[]{:S(2)}) copy-start(f32[2,128,4096]{2,1,0:T(8,128)} %reshape.54) | copy-start | bytes 12582916
  631.6 10.1 %copy-start.4 = (bf16[2,128,4096]{2,1,0:T(8,128)(2,1)S(1)}, bf16[2,128,4096]{2,1,0:T(8,128)(2,1)}, u32[]{:S(2)}) copy-start(bf16[2,128,4096]{2,1,0:T(8,128)(2,1)} %param.14) | copy-start | bytes 6291460
  631.6 11.3 %copy-start.9 = (f32[2,128,4096]{2,1,0:T(8,128)S(1)}, f32[2,128,4096]{2,1,0:T(8,128)}, u32[]{:S(2)}) copy-start(f32[2,128,4096]{2,1,0:T(8,128)} %param.20) | copy-start | bytes 12582916
  631.6 12.5 %copy-start.10 = (f32[2,128,4096]{2,1,0:T(8,128)S(1)}, f32[2,128,4096]{2,1,0:T(8,128)}, u32[]{:S(2)}) copy-start(f32[2,128,4096]{2,1,0:T(8,128)} %param.17) | copy-start | bytes 12582916
  644.1 5.6 copy-start
  644.1 6.1 copy-start.6
  644.1 7.7 %copy-start.11 = (f32[2,512,1024]{2,1,0:T(8,128)S(1)}, f32[2,512,1024]{2,1,0:T(8,128)}, u32[]{:S(2)}) copy-start(f32[2,512,1024]{2,1,0:T(8,128)} %param.21) | copy-start | bytes 12582916
  644.2 8.9 %copy-start.12 = (f32[2,512,1024]{2,1,0:T(8,128)S(1)}, f32[2,512,1024]{2,1,0:T(8,128)}, u32[]{:S(2)}) copy-start(f32[2,512,1024]{2,1,0:T(8,128)} %param.18) | copy-start | bytes 12582916

commit v2 on v1

--- a/solution.py
+++ b/solution.py
@@ -14,7 +14,11 @@
 CH = 512
 BM = 512
 EPS = 1e-6
+OWN_SLOTS = 8
+LEAD = 2
 COMM = True
+AG = True
+RS = True
 COMPUTE = True
 
 
@@ -31,9 +35,9 @@
 
 
 def kernel(
-    chips, layers, groups, x, dy, own, gout, agb, part, save,
-    A0, A1, H, DY, ACC, WGU, WD, HID, DG, DU, ST, DWS, DWD, R0, PB, C, F, Q, G,
-    in_sem, ag_send, ag_relay, ag_l, ag_r, ag_o, ag_p, ag_loc, w_sem, st_sem, dw_sem,
+    chips, layers, groups, x, dy, wg, wu, wd, gg, gu, gd, agb, part, save,
+    A0, A1, H, DY, ACC, WGU, WD, HID, DG, DU, ST, DWS, DWD, R0, PB, C, F, Q, G, OWN,
+    in_sem, own_sem, ag_send, ag_relay, ag_l, ag_r, ag_o, ag_p, ag_loc, w_sem, st_sem, dw_sem,
     s0, r0, lp, ss, rc, rf, g_sem, credit0, credit_l, credit_r,
 ):
     tokens, d = x.shape
@@ -55,10 +59,45 @@
             return (lambda f: f()) if cond else (lambda f: None)
         return pl.when(cond)
 
+    def place(t):
+        rest = lax.rem(t, per_layer)
+        return t // per_layer, rest // 3, lax.rem(rest, 3)
+
+    def gu_cols(y, parity, q):
+        return pl.ds(pl.multiple_of(((2 * y + parity) * groups + q) * R, R), R)
+
+    def own_load(p):
+        layer, q, k = place(p)
+        s = lax.rem(p, OWN_SLOTS)
+
+        @pl.when(k == 0)
+        def _():
+            for half in range(2):
+                src = wd.at[layer, pl.ds(pl.multiple_of(q * R, R), R), half * CH : (half + 1) * CH]
+                local(src, OWN.at[s, half], own_sem.at[s]).start()
+
+        @pl.when(k > 0)
+        def _():
+            for which, w in enumerate((wg, wu)):
+                for y in range(chips):
+                    local(w.at[layer, :, gu_cols(y, k - 1, q)], OWN.at[s, which, :, y * R : (y + 1) * R], own_sem.at[s]).start()
+
+    def sent(p):
+        four = agb.at[p, :, 0]
+        remote(four, four, ag_send.at[p], ag_p.at[p], partner).wait_send()
+
     def e0(p):
+        s = lax.rem(p, OWN_SLOTS)
+        local(agb.at[p, 0, 0], OWN.at[s], own_sem.at[s]).wait()
         for to, sem in ((right, ag_l), (left, ag_r), (partner, ag_p)):
-            remote(own.at[p], agb.at[p, X, c], ag_send.at[p], sem.at[p], to).start()
-        local(own.at[p], agb.at[p, X, c], ag_loc.at[p]).start()
+            remote(OWN.at[s], agb.at[p, X, c], ag_send.at[p], sem.at[p], to).start()
+        local(OWN.at[s], agb.at[p, X, c], ag_loc.at[p]).start()
+        ahead = p + 2
+
+        @pl.when(ahead < packets)
+        def _():
+            pl.when(ahead >= OWN_SLOTS)(lambda: sent(ahead - OWN_SLOTS))
+            own_load(ahead)
 
     def e1(p):
         remote(agb.at[p, XL, c], agb.at[p, XL, c], ag_send.at[p], ag_l.at[p], right).wait_recv()
@@ -73,27 +112,30 @@
         remote(agb.at[p, XO, c], agb.at[p, XO, c], ag_relay.at[p], ag_p.at[p], partner).start()
 
     def ready(p):
-        if not COMM:
+        if not AG:
             return
         everyone = agb.at[p, :, 1 - c]
         remote(everyone, everyone, ag_relay.at[p], ag_p.at[p], partner).wait_recv()
-        local(own.at[p], agb.at[p, X, c], ag_loc.at[p]).wait()
+        local(OWN.at[0], agb.at[p, X, c], ag_loc.at[p]).wait()
 
     def ag_tick(a):
-        if not COMM:
+        if not AG:
             return
-        when(a < packets)(lambda: e0(a))
-        when((a >= 2) & (a < packets + 2) if not isinstance(a, int) else 2 <= a < packets + 2)(lambda: e1(a - 2))
-        when((a >= 3) & (a < packets + 3) if not isinstance(a, int) else 3 <= a < packets + 3)(lambda: e2(a - 3))
+        def at(k, do):
+            when(0 <= k < packets if isinstance(k, int) else (k >= 0) & (k < packets))(lambda: do(k))
+
+        at(a, e0)
+        at(a - LEAD, e1)
+        at(a - LEAD - 1, e2)
 
     def ag_drain():
-        if not COMM:
+        if not AG:
             return
 
         @pl.loop(0, packets)
         def _(p):
-            four, three = agb.at[p, :, 0], agb.at[p, pl.ds(0, 3), 0]
-            remote(four, four, ag_send.at[p], ag_p.at[p], partner).wait_send()
+            three = agb.at[p, pl.ds(0, 3), 0]
+            pl.when(p >= packets - OWN_SLOTS)(lambda: sent(p))
             remote(three, three, ag_relay.at[p], ag_p.at[p], partner).wait_send()
 
     def rs0(t):
@@ -150,14 +192,33 @@
         for send in seconds(s):
             remote(*send).start()
 
+    def g_wait(g):
+        local(G.at[g], agb.at[0, 0, 0], g_sem.at[g]).wait()
+
+    def g_out(t, g):
+        backward, q, k = place(t)
+        layer = layers - 1 - backward
+
+        @pl.when(k == 2)
+        def _():
+            for half in range(2):
+                dst = gd.at[layer, pl.ds(pl.multiple_of(q * R, R), R), half * CH : (half + 1) * CH]
+                local(G.at[g, half], dst, g_sem.at[g]).start()
+
+        @pl.when(k < 2)
+        def _():
+            for which, out in enumerate((gg, gu)):
+                for y in range(chips):
+                    local(G.at[g, which, :, y * R : (y + 1) * R], out.at[layer, :, gu_cols(y, k, q)], g_sem.at[g]).start()
+
     def rs3(t):
         s, g = lax.rem(t, 4), lax.rem(t, 2)
         for send in firsts(s)[2:] + seconds(s):
             remote(*send).wait_recv()
-        pl.when(t >= 2)(lambda: local(G.at[g], gout.at[t - 2], g_sem.at[g]).wait())
+        pl.when(t >= 2)(lambda: g_wait(g))
         plus(G.at[g, 0], PB.at[s, X, 0], F.at[s, 1], F.at[s, 2])
         plus(G.at[g, 1], PB.at[s, X, 1], F.at[s, 0], F.at[s, 3])
-        local(G.at[g], gout.at[t], g_sem.at[g]).start()
+        g_out(t, g)
         for send in firsts(s) + seconds(s):
             remote(*send).wait_send()
         remote(part.at[t, :, 1 - c], R0.at[s], s0.at[s], r0.at[s], partner).wait_send()
@@ -168,7 +229,7 @@
             pl.semaphore_signal(credit_l, 1, device_id=right, device_id_type=MESH)
 
     def rs_tick(k):
-        if not COMM:
+        if not RS:
             return
         pl.when((k >= 0) & (k < packets))(lambda: rs0(k))
         pl.when((k >= 1) & (k < packets + 1))(lambda: rs1(k - 1))
@@ -253,39 +314,51 @@
     load_x, load_dy = local(x, H, in_sem.at[0]), local(dy, DY, in_sem.at[1])
     load_x.start()
     load_dy.start()
+    if AG:
+        own_load(0)
+        own_load(1)
     ag_tick(0)
     ag_tick(1)
     load_x.wait()
     normed(H, A0)
     ACC[...] = jnp.zeros_like(ACC)
     load_dy.wait()
-    ag_tick(2)
+    for a in range(2, LEAD + 3):
+        ag_tick(a)
+    ready(0)
+    ready(1)
+    if COMPUTE:
+        gu_load(0, 0, 0).start()
+        down_load(0, 0, 0).start()
 
     def saved(b, slot, out):
         if out:
             return local(ST.at[slot], save.at[b], st_sem.at[slot])
         return local(save.at[b], ST.at[slot], st_sem.at[slot])
 
+    def fetch(layer, j, slot):
+        p = p_gu(layer, j)
+        pl.when(lax.rem(j, 2) == 0)(lambda: ready(p - 1))
+        ready(p)
+        if COMPUTE:
+            gu_load(layer, j, slot).start()
+            down_load(layer, j, slot).start()
+
     @pl.loop(0, chunks)
     def _(i):
         slot = lax.rem(i, 2)
-        p = p_gu(0, i)
-
-        @pl.when(slot == 0)
-        def _():
-            ag_tick(p + 2)
-            ready(p - 1)
-
-        ag_tick(p + 3)
-        ready(p)
+        following = i + 1
+        p = per_layer * (following // chunks) + 3 * (lax.rem(following, chunks) // 2) + 1 + lax.rem(following, 2)
         if COMPUTE:
-            gu_load(0, i, slot).start()
-            down_load(0, i, slot).start()
             gu_load(0, i, slot).wait()
             down_load(0, i, slot).wait()
 
-            @pl.loop(0, blocks)
-            def _(r):
+        @pl.loop(0, blocks)
+        def _(r):
+            pl.when((r == 0) & (slot == 1))(lambda: ag_tick(p + LEAD))
+            pl.when(r == 1)(lambda: ag_tick(p + LEAD + 1))
+            pl.when((r == blocks - 1) & (following < chunks))(lambda: fetch(0, following, 1 - slot))
+            if COMPUTE:
                 rows = rows_of(r)
                 b = i * blocks + r
                 ss_ = lax.rem(b, 2)
@@ -305,8 +378,7 @@
     if COMPUTE:
         for b in (last - 2, last - 1):
             saved(b, b % 2, True).wait()
-    ag_tick(per_layer + 3)
-    if COMPUTE:
+
         @pl.loop(0, tokens // 256)
         def _(b):
             rows = pl.ds(pl.multiple_of(b * 256, 256), 256)
@@ -316,12 +388,7 @@
             scale = lax.rsqrt(jnp.mean(wide * wide, -1, keepdims=True) + EPS)
             A1[rows, :] = (wide * scale).astype(BF16)
             ACC[rows, :] = jnp.zeros((256, d), F32)
-    ag_tick(per_layer + 4)
-    ready(per_layer)
-    ready(per_layer + 1)
-    if COMPUTE:
-        gu_load(1, 0, 0).start()
-        down_load(1, 0, 0).start()
+    fetch(1, jnp.int32(0), 0)
 
     @pl.loop(0, chunks)
     def _(i):
@@ -329,31 +396,28 @@
         if COMPUTE:
             gu_load(1, i, slot).wait()
             down_load(1, i, slot).wait()
-        ag_tick(per_layer + 5 + 2 * i)
-
-        @pl.when(i + 1 < chunks)
-        def _():
-            p = p_gu(1, i + 1)
-            pl.when(slot == 1)(lambda: ready(p - 1))
-            ready(p)
+
+        @pl.loop(0, blocks)
+        def _(r):
+            pl.when(r == 0)(lambda: ag_tick(per_layer + 3 + LEAD + 2 * i))
+            pl.when(r == 2)(lambda: ag_tick(per_layer + 4 + LEAD + 2 * i))
+
+            @pl.when((r == 1) & (i >= 1))
+            def _():
+                if COMPUTE:
+                    settle(i - 1)
+                rs_tick(unit_gu(i - 1))
+
+            pl.when((r == 3) & (i >= 1) & (slot == 0))(lambda: rs_tick(unit_down(i - 1)))
             if COMPUTE:
-                gu_load(1, i + 1, 1 - slot).start()
-                down_load(1, i + 1, 1 - slot).start()
-
-        if COMPUTE:
-            @pl.loop(0, blocks)
-            def _(r):
                 rows = rows_of(r)
                 a = A1[rows, :]
                 through(nn(a, w_in(slot, 0)), nn(a, w_in(slot, 1)), by_hidden(slot, rows), rows)
                 ACC[rows, :] += nt(DG[rows, :], w_in(slot, 0)) + nt(DU[rows, :], w_in(slot, 1))
 
-            pl.when(i >= 1)(lambda: settle(i - 1))
-        pl.when(i >= 1)(lambda: rs_tick(unit_gu(i - 1)))
-        ag_tick(per_layer + 6 + 2 * i)
+        pl.when(i + 1 < chunks)(lambda: fetch(1, i + 1, 1 - slot))
         if COMPUTE:
             gradients(A1, unit_gu(i), unit_down(i), i)
-        pl.when((i >= 1) & (slot == 0))(lambda: rs_tick(unit_down(i - 1)))
 
     if COMPUTE:
         down_load(0, 0, 0).start()
@@ -378,8 +442,16 @@
             down_load(0, i, slot).wait()
             pl.when(i + 1 < chunks)(lambda: down_load(0, i + 1, 1 - slot).start())
 
-            @pl.loop(0, blocks)
-            def _(r):
+        @pl.loop(0, blocks)
+        def _(r):
+            @pl.when(r == 1)
+            def _():
+                if COMPUTE:
+                    settle(k - 1)
+                rs_tick(unit_gu(k - 1))
+
+            pl.when((r == 3) & (slot == 0))(lambda: rs_tick(unit_down(k - 1)))
+            if COMPUTE:
                 rows = rows_of(r)
                 b = i * blocks + r
                 ss_ = lax.rem(b, 2)
@@ -387,11 +459,8 @@
                 through(ST[ss_, 0], ST[ss_, 1], by_hidden(slot, rows), rows)
                 pl.when(b + 2 < last)(lambda: saved(b + 2, ss_, False).start())
 
-            settle(k - 1)
-        rs_tick(unit_gu(k - 1))
         if COMPUTE:
             gradients(A0, unit_gu(k), unit_down(k), i)
-        pl.when(slot == 0)(lambda: rs_tick(unit_down(k - 1)))
 
     if COMPUTE:
         settle(2 * chunks - 1)
@@ -400,18 +469,18 @@
     def _(k):
         rs_tick(k)
 
-    if COMM:
+    if RS:
         for t in (packets - 2, packets - 1):
-            local(G.at[t % 2], gout.at[t], g_sem.at[t % 2]).wait()
+            g_wait(t % 2)
     ag_drain()
 
 
-def gradients_of(mesh, x, dy, own):
+def gradients_of(mesh, x, dy, wg, wu, wd):
     chips = mesh.shape["dp"] // 2
-    packets = own.shape[0]
     tokens, d = x.shape
-    layers = 2
-    groups = packets // layers // 3
+    layers, hidden, _ = wd.shape
+    groups = hidden // R
+    packets = layers * 3 * groups
     unit = (2, R, CH)
     dma, reg = pltpu.SemaphoreType.DMA, pltpu.SemaphoreType.REGULAR
     V = pltpu.VMEM
@@ -421,27 +490,27 @@
     return pl.pallas_call(
         functools.partial(kernel, chips, layers, groups),
         out_shape=(
-            jax.ShapeDtypeStruct((packets, *unit), BF16),
+            *(jax.ShapeDtypeStruct(w.shape, BF16) for w in (wg, wu, wd)),
             jax.ShapeDtypeStruct((packets, chips, 2, *unit), BF16),
             jax.ShapeDtypeStruct((packets, chips, 2, *unit), BF16),
             jax.ShapeDtypeStruct((chunks * blocks, 2, BM, CH), F32),
         ),
-        in_specs=[hbm] * 3,
-        out_specs=(hbm,) * 4,
+        in_specs=[hbm] * 5,
+        out_specs=(hbm,) * 6,
         scratch_shapes=[
             V((tokens, d), BF16), V((tokens, d), BF16), V((tokens, d), BF16), V((tokens, d), BF16), V((tokens, d), F32),
             V((2, chips, 2, *unit), BF16), V((2, chips, *unit), BF16),
             V((tokens, CH), BF16), V((tokens, CH), BF16), V((tokens, CH), BF16),
             V((2, 2, BM, CH), F32), V((chips, 2, *unit), BF16), V((chips, *unit), BF16),
             V((4, chips, *unit), BF16), V((4, chips, *unit), BF16), V((4, *unit), BF16), V((4, 4, R, CH), BF16), V((4, *unit), BF16),
-            V((2, *unit), BF16),
-            dma((2,)), *[dma((packets,))] * 7, dma((2, 2)), dma((2,)), dma((2,)),
+            V((2, *unit), BF16), V((OWN_SLOTS, *unit), BF16),
+            dma((2,)), dma((OWN_SLOTS,)), *[dma((packets,))] * 7, dma((2, 2)), dma((2,)), dma((2,)),
             dma((4,)), dma((4,)), dma((4,)), dma((4, 6)), dma((4, 2)), dma((4, 4)), dma((2,)), reg, reg, reg,
         ],
-        compiler_params=pltpu.CompilerParams(collective_id=0, has_side_effects=True, vmem_limit_bytes=67043328),
+        compiler_params=pltpu.CompilerParams(collective_id=0 if COMM else None, has_side_effects=True, vmem_limit_bytes=67043328),
         cost_estimate=pl.CostEstimate(flops=flops, bytes_accessed=300 << 20, transcendentals=0),
         name="step",
-    )(x, dy, own)[0]
+    )(x, dy, wg, wu, wd)[:3]
 
 
 def adamw(w, m, v, g):
@@ -452,27 +521,9 @@
 
 
 def solution(mesh):
-    chips = mesh.shape["dp"] // 2
-
     def step(x, dy, *arrays):
         weights, m, v = (arrays[i : i + 3] for i in (0, 3, 6))
-        layers, _, ff = weights[0].shape
-        d = weights[2].shape[2]
-        groups = ff // (2 * chips) // R
-
-        def spread(w):
-            return w.reshape(layers, R, chips, 2, groups, R).transpose(0, 4, 3, 1, 2, 5).reshape(layers, groups, 2, R, CH)
-
-        gu = jnp.stack([spread(weights[0]), spread(weights[1])], 3)
-        down = weights[2].reshape(layers, groups, R, 2, CH).transpose(0, 1, 3, 2, 4)
-        own = jnp.concatenate([down[:, :, None], gu], 2).reshape(-1, 2, R, CH)
-        g = gradients_of(mesh, x[0], dy[0], own).reshape(layers, groups, 3, 2, R, CH)[::-1]
-
-        def gathered(which):
-            return g[:, :, :2, which].reshape(layers, groups, 2, R, chips, R).transpose(0, 3, 4, 2, 1, 5).reshape(layers, R, ff)
-
-        g_down = g[:, :, 2].transpose(0, 1, 3, 2, 4).reshape(layers, groups * R, d)
-        gradients = [one.astype(jnp.float32) for one in (gathered(0), gathered(1), g_down)]
+        gradients = [one.astype(jnp.float32) for one in gradients_of(mesh, x[0], dy[0], *weights)]
         new = [adamw(w.astype(jnp.float32), m, v, g) for w, m, v, g in zip(weights, m, v, gradients, strict=True)]
         return tuple(one[which] for which in range(3) for one in new)
 

time: 665 us -> 525 us (0.79); the launches traced: 658 us -> 525 us
  local copies, waits for them, and re-layouts: 89.2 us -> 1.95 us
  Pallas kernels: 538 us -> 500 us
  other arithmetic: 30.1 us -> 22.2 us
    convert_element_type x8 -> x0, local copies, waits for them, and re-layouts: 47.4 us -> none  [step(): one.astype(jnp.float32)]
    pallas_call x1, Pallas kernels: 538 us -> 500 us  [gradients_of(): pl.pallas_call(functools.partial(kernel, chips, layers, groups), out_shap...]
    reshape x4 -> x0, local copies, waits for them, and re-layouts: 12 us -> none  [the longest x2 7.12 us: spread(): w.reshape(layers, R, chips, 2, groups, R).transpose(0, 4, 3, 1, 2, 5)]
    another operation x2 -> x0, local copies, waits for them, and re-layouts: 8.2 us -> none  [step(): gu = jnp.stack([spread(weights[0]), spread(weights[1])], 3)]
    transpose x2 -> x0, local copies, waits for them, and re-layouts: 8.14 us -> none  [spread(): w.reshape(layers, R, chips, 2, groups, R).transpose(0, 4, 3, 1, 2, 5)]
    convert_element_type x2 -> x0, other arithmetic: 6.74 us -> none  [step(): one.astype(jnp.float32)]
    convert_element_type x3 -> x2, other arithmetic: 19.1 us -> 22.2 us  [adamw(): return ((w - 0.02 * step).astype(jnp.bfloat16), m, v)]
where the time goes in v2:
time: 525 us
  Pallas kernels  500 us (95%)
  other arithmetic  22.2 us (4%)
    pallas_call x1, Pallas kernels, gradients_of(): pl.pallas_call(functools.partial(kernel, chips, layers, groups), out_shap...  500 us
    convert_element_type x2, other arithmetic, adamw(): return ((w - 0.02 * step).astype(jnp.bfloat16), m, v)  22.2 us

profile of v2, /device:TPU:112, one launch (start us, length us, event | category | flops | bytes accessed | tf_op | source)
XLA Modules:
  0.0 524.9 jit_solution(2606009526244531620)
XLA Ops:
  0.6 500.0 %step.1 = (bf16[2,128,4096]{2,1,0:T(8,128)(2,1)}, bf16[2,128,4096]{2,1,0:T(8,128)(2,1)}, bf16[2,512,1024]{2,1,0:T(8,128)(2,1)}, bf16[24,4,2,2,128,512]{5,4,3,2,1...) custom-call(bf16[2048,1024]{1,0:T(8,128)(2,1)} %bitcast.2, ...), custom_call_target="tpu_custom_call" | custom-call | flops 257698037760 | bytes 314572800 | tf_op jit(solution)/shard_map/step/pallas_call | solution.py:490
  500.6 0.0 copy-start
  500.6 0.0 copy-start.1
  500.6 8.8 %fusion.10 = (bf16[2,512,1024]{2,1,0:T(8,128)(2,1)}, f32[2,512,1024]{2,1,0:T(8,128)}, f32[2,512,1024]{2,1,0:T(8,128)}) fusion(bf16[2,512,1024]{2,1,0:T(8,128)(2,1)} %wd.1, bf16[2,512,1024]{2,1,0:T(8,128)(2,1)} %get-tuple-element.14, f32[2,512,1024]{2,1,0:T(8,128)} %param.21, f32[2,512,1024]{2,1,0:T(8,128)} %param.18), kind=kLoop, calls=%fused_computation.22 | loop fusion | flops 16777216 | bytes 23068672 | tf_op jit(solution)/shard_map/convert_element_type | solution.py:520
  509.4 0.1 copy-done
  509.5 1.9 copy-done.1
  511.3 13.4 %fusion.2 = (bf16[2,128,4096]{2,1,0:T(8,128)(2,1)}, f32[2,128,4096]{2,1,0:T(8,128)}, f32[2,128,4096]{2,1,0:T(8,128)}, bf16[2,128,4096]{2,1,0:T(8,128)(2,1)}, f32...) fusion(bf16[2,128,4096]{2,1,0:T(8,128)(2,1)} %wg.1, bf16[2,128,4096]{2,1,0:T(8,128)(2,1)} %get-tuple-element.12, ...), kind=kLoop, calls=%fused_computation.14 | loop fusion | flops 33554432 | bytes 46137344 | tf_op jit(solution)/shard_map/convert_element_type | solution.py:520
Async XLA Ops:
  500.6 8.9 %copy-start = (f32[2,128,4096]{2,1,0:T(8,128)S(1)}, f32[2,128,4096]{2,1,0:T(8,128)}, u32[]{:S(2)}) copy-start(f32[2,128,4096]{2,1,0:T(8,128)} %param.19) | copy-start | bytes 12582916
  500.6 10.7 %copy-start.1 = (f32[2,128,4096]{2,1,0:T(8,128)S(1)}, f32[2,128,4096]{2,1,0:T(8,128)}, u32[]{:S(2)}) copy-start(f32[2,128,4096]{2,1,0:T(8,128)} %param.16) | copy-start | bytes 12582916

commit v3 on v2

--- a/solution.py
+++ b/solution.py
@@ -14,7 +14,7 @@
 CH = 512
 BM = 512
 EPS = 1e-6
-OWN_SLOTS = 8
+OWN_SLOTS = 10
 LEAD = 2
 COMM = True
 AG = True
@@ -199,17 +199,17 @@
         backward, q, k = place(t)
         layer = layers - 1 - backward
 
-        @pl.when(k == 2)
+        @pl.when(k == 1)
         def _():
             for half in range(2):
                 dst = gd.at[layer, pl.ds(pl.multiple_of(q * R, R), R), half * CH : (half + 1) * CH]
                 local(G.at[g, half], dst, g_sem.at[g]).start()
 
-        @pl.when(k < 2)
+        @pl.when(k != 1)
         def _():
             for which, out in enumerate((gg, gu)):
                 for y in range(chips):
-                    local(G.at[g, which, :, y * R : (y + 1) * R], out.at[layer, :, gu_cols(y, k, q)], g_sem.at[g]).start()
+                    local(G.at[g, which, :, y * R : (y + 1) * R], out.at[layer, :, gu_cols(y, k // 2, q)], g_sem.at[g]).start()
 
     def rs3(t):
         s, g = lax.rem(t, 4), lax.rem(t, 2)
@@ -228,13 +228,18 @@
             pl.semaphore_signal(credit_r, 1, device_id=left, device_id_type=MESH)
             pl.semaphore_signal(credit_l, 1, device_id=right, device_id_type=MESH)
 
+    def rs_rest(k):
+        if not RS:
+            return
+        pl.when((k >= 1) & (k < packets + 1))(lambda: rs1(k - 1))
+        pl.when((k >= 2) & (k < packets + 2))(lambda: rs2(k - 2))
+        pl.when((k >= 3) & (k < packets + 3))(lambda: rs3(k - 3))
+
     def rs_tick(k):
         if not RS:
             return
-        pl.when((k >= 0) & (k < packets))(lambda: rs0(k))
-        pl.when((k >= 1) & (k < packets + 1))(lambda: rs1(k - 1))
-        pl.when((k >= 2) & (k < packets + 2))(lambda: rs2(k - 2))
-        pl.when((k >= 3) & (k < packets + 3))(lambda: rs3(k - 3))
+        pl.when(k < packets)(lambda: rs0(k))
+        rs_rest(k)
 
     def p_down(layer, j):
         return layer * per_layer + 3 * (j // 2)
@@ -290,6 +295,16 @@
             DWD[:, half] = g.astype(BF16).reshape(chips, R, CH)
         part_down(t_down, j).start()
         for b in range(d // 256):
+            if b == 1:
+                @pl.when(lax.rem(j, 2) == 1)
+                def _():
+                    part_down(t_down, j).wait()
+                    if RS:
+                        rs0(t_down)
+                    pl.when(t_down < packets - 2)(lambda: rs_rest(t_down))
+
+            if b == 3:
+                pl.when(t == packets - 1)(lambda: rs_rest(t))
             cols = slice(256 * b, 256 * b + 256)
             for which, by in ((0, DG), (1, DU)):
                 g = tn(A[:, cols], by[...])
@@ -297,14 +312,14 @@
         part_out(t).start()
 
     def unit_gu(k):
-        return 3 * (k // 2) + lax.rem(k, 2)
+        return 3 * (k // 2) + 2 * lax.rem(k, 2)
 
     def unit_down(k):
-        return 3 * (k // 2) + 2
+        return 3 * (k // 2) + 1
 
     def settle(k):
         part_out(unit_gu(k)).wait()
-        part_down(unit_down(k), k).wait()
+        pl.when(lax.rem(k, 2) == 0)(lambda: part_down(unit_down(k), k).wait())
 
     if COMM:
         barrier = pltpu.get_barrier_semaphore()
@@ -399,8 +414,10 @@
 
         @pl.loop(0, blocks)
         def _(r):
-            pl.when(r == 0)(lambda: ag_tick(per_layer + 3 + LEAD + 2 * i))
-            pl.when(r == 2)(lambda: ag_tick(per_layer + 4 + LEAD + 2 * i))
+            first = per_layer + 3 + LEAD
+            early = i < 2
+            pl.when(early & (r != 1))(lambda: ag_tick(first + 3 * i + jnp.maximum(r - 1, 0)))
+            pl.when((i >= 2) & (r == 0))(lambda: ag_tick(first + 4 + i))
 
             @pl.when((r == 1) & (i >= 1))
             def _():
@@ -408,7 +425,6 @@
                     settle(i - 1)
                 rs_tick(unit_gu(i - 1))
 
-            pl.when((r == 3) & (i >= 1) & (slot == 0))(lambda: rs_tick(unit_down(i - 1)))
             if COMPUTE:
                 rows = rows_of(r)
                 a = A1[rows, :]
@@ -450,7 +466,7 @@
                     settle(k - 1)
                 rs_tick(unit_gu(k - 1))
 
-            pl.when((r == 3) & (slot == 0))(lambda: rs_tick(unit_down(k - 1)))
+            pl.when((r == 3) & (i == chunks - 1))(lambda: rs_rest(unit_gu(k - 1) + 1))
             if COMPUTE:
                 rows = rows_of(r)
                 b = i * blocks + r
@@ -463,11 +479,13 @@
             gradients(A0, unit_gu(k), unit_down(k), i)
 
     if COMPUTE:
-        settle(2 * chunks - 1)
-
-    @pl.loop(packets - 2, packets + 3)
-    def _(k):
-        rs_tick(k)
+        settle(jnp.int32(2 * chunks - 1))
+    if RS:
+        rs0(jnp.int32(packets - 1))
+
+        @pl.loop(packets, packets + 3)
+        def _(k):
+            rs_rest(k)
 
     if RS:
         for t in (packets - 2, packets - 1):

time: 525 us -> 525 us (level)
  no operation moved by 1% of the time
where the time goes in v3:
time: 525 us
  Pallas kernels  500 us (95%)
  other arithmetic  22.2 us (4%)
    pallas_call x1, Pallas kernels, gradients_of(): pl.pallas_call(functools.partial(kernel, chips, layers, groups), out_shap...  500 us
    convert_element_type x2, other arithmetic, adamw(): return ((w - 0.02 * step).astype(jnp.bfloat16), m, v)  22.2 us

profile of v3, /device:TPU:112, one launch (start us, length us, event | category | flops | bytes accessed | tf_op | source)
XLA Modules:
  0.0 525.2 jit_solution(2987482176745345559)
XLA Ops:
  0.6 500.3 %step.1 = (bf16[2,128,4096]{2,1,0:T(8,128)(2,1)}, bf16[2,128,4096]{2,1,0:T(8,128)(2,1)}, bf16[2,512,1024]{2,1,0:T(8,128)(2,1)}, bf16[24,4,2,2,128,512]{5,4,3,2,1...) custom-call(bf16[2048,1024]{1,0:T(8,128)(2,1)} %bitcast.2, ...), custom_call_target="tpu_custom_call" | custom-call | flops 257698037760 | bytes 314572800 | tf_op jit(solution)/shard_map/step/pallas_call | solution.py:508
  500.9 0.0 copy-start
  500.9 0.0 copy-start.1
  501.0 8.8 %fusion.10 = (bf16[2,512,1024]{2,1,0:T(8,128)(2,1)}, f32[2,512,1024]{2,1,0:T(8,128)}, f32[2,512,1024]{2,1,0:T(8,128)}) fusion(bf16[2,512,1024]{2,1,0:T(8,128)(2,1)} %wd.1, bf16[2,512,1024]{2,1,0:T(8,128)(2,1)} %get-tuple-element.14, f32[2,512,1024]{2,1,0:T(8,128)} %param.21, f32[2,512,1024]{2,1,0:T(8,128)} %param.18), kind=kLoop, calls=%fused_computation.22 | loop fusion | flops 16777216 | bytes 23068672 | tf_op jit(solution)/shard_map/convert_element_type | solution.py:538
  509.7 0.1 copy-done
  509.8 1.9 copy-done.1
  511.7 13.5 %fusion.2 = (bf16[2,128,4096]{2,1,0:T(8,128)(2,1)}, f32[2,128,4096]{2,1,0:T(8,128)}, f32[2,128,4096]{2,1,0:T(8,128)}, bf16[2,128,4096]{2,1,0:T(8,128)(2,1)}, f32...) fusion(bf16[2,128,4096]{2,1,0:T(8,128)(2,1)} %wg.1, bf16[2,128,4096]{2,1,0:T(8,128)(2,1)} %get-tuple-element.12, ...), kind=kLoop, calls=%fused_computation.14 | loop fusion | flops 33554432 | bytes 46137344 | tf_op jit(solution)/shard_map/convert_element_type | solution.py:538
Async XLA Ops:
  500.9 8.9 %copy-start = (f32[2,128,4096]{2,1,0:T(8,128)S(1)}, f32[2,128,4096]{2,1,0:T(8,128)}, u32[]{:S(2)}) copy-start(f32[2,128,4096]{2,1,0:T(8,128)} %param.19) | copy-start | bytes 12582916
  500.9 10.7 %copy-start.1 = (f32[2,128,4096]{2,1,0:T(8,128)S(1)}, f32[2,128,4096]{2,1,0:T(8,128)}, u32[]{:S(2)}) copy-start(f32[2,128,4096]{2,1,0:T(8,128)} %param.16) | copy-start | bytes 12582916
